TPU v7x, 32 devices: a whole 2x2x4 slice. The times are simulated.
32 devices in a mesh: dp: 8 (over z, x), tp: 4 (over y, core).
Axes of the slice: x: 2, y: 2, z: 4, core: 2. Of those that a mesh axis runs over, the one named last changes fastest.
Arguments:
- queries: bfloat16 [4096, 8192], P('dp', 'tp'), parts along dimension 0, may hold values from -200 to 200
- new_keys: bfloat16 [4096, 1024], P('dp', 'tp'), parts along dimension 0, may hold values from -9 to 9
- new_values: bfloat16 [4096, 1024], P('dp', 'tp'), parts along dimension 0, may hold values from -60 to 60
- cache_keys: bfloat16 [32, 32768, 128], P('dp', 'tp'), parts along dimension 0, may hold values from -4 to 4
- cache_values: bfloat16 [32, 32768, 128], P('dp', 'tp'), parts along dimension 0, may hold values from -60 to 60
- out_weight: bfloat16 [8192, 8192], P('tp'), may hold values from -0.09375 to 0.09375
- residual: bfloat16 [4096, 8192], P('dp', 'tp'), parts along dimension 0, may hold values from -8 to 8
- norm_gain: bfloat16 [8192], P('tp'), may hold values from 0.5 to 1.5
Outputs:
- normed: bfloat16 [4096, 8192], P('dp', 'tp'), parts along dimension 0
There are 8 independent parts, one for each index of `dp`. A program takes and returns all parts, laid end to end along the dimension named above; an argument that names none is the same for every part. Nothing has to cross between parts.
All inputs are finite; a program needn't handle non-finite values.
Results may differ from a plain program's by a relative error of at most 0.015.
Values may be sent and summed in bfloat16 or wider, within the bound.
A program may use at most 256 MiB of HBM per device.

v0:
```python
import functools

import jax
import jax.numpy as jnp
from jax import lax
from jax.experimental import pallas as pl
from jax.experimental.pallas import tpu as pltpu
from jax.sharding import PartitionSpec as P

D = 8192
KVH = 8
HD = 128
SPAN = 128
SEQS = 4
CTX = 4096


EPSILON = 1e-05


def partner(value, axis, bit):
    mask = 2**bit
    pairs = [(source, source ^ mask) for source in range(lax.axis_size(axis))]
    return lax.ppermute(value, axis, pairs)


def attend_block(query_rows, stored_keys, stored_values, fresh_keys, fresh_values, local_kv):
    heads_here = query_rows.shape[1] // HD
    groups = heads_here // local_kv
    length = stored_keys.shape[1] // local_kv
    scaling = HD ** (-0.5)
    grouped = query_rows.reshape(SEQS, SPAN, local_kv, groups, HD)
    old_keys = stored_keys.reshape(SEQS, local_kv, length, HD)
    old_values = stored_values.reshape(SEQS, local_kv, length, HD)
    scores = (
        jnp.einsum("sighd,sgjd->sghij", grouped, old_keys, preferred_element_type=jnp.float32)
        * scaling
    )
    peak = jnp.max(scores, axis=-1)
    recent_keys = fresh_keys.reshape(SEQS, SPAN, local_kv, HD)
    recent_values = fresh_values.reshape(SEQS, SPAN, local_kv, HD)
    recent_scores = (
        jnp.einsum("sighd,sjgd->sghij", grouped, recent_keys, preferred_element_type=jnp.float32)
        * scaling
    )
    causal = jnp.arange(SPAN)[:, None] >= jnp.arange(SPAN)[None, :]
    recent_scores = jnp.where(causal, recent_scores, -jnp.inf)
    peak = jnp.maximum(peak, jnp.max(recent_scores, axis=-1))
    weights = jnp.exp(scores - peak[..., None])
    total = jnp.sum(weights, axis=-1)
    mixed = jnp.einsum(
        "sghij,sgjd->sighd",
        weights.astype(jnp.bfloat16),
        old_values,
        preferred_element_type=jnp.float32,
    )
    recent_weights = jnp.exp(recent_scores - peak[..., None])
    total = total + jnp.sum(recent_weights, axis=-1)
    mixed = mixed + jnp.einsum(
        "sghij,sjgd->sighd",
        recent_weights.astype(jnp.bfloat16),
        recent_values,
        preferred_element_type=jnp.float32,
    )
    return (mixed, peak, total)


def token_layout(stat):
    return jnp.transpose(stat, (0, 3, 1, 2))[..., None]


def finish_rows(mixed, total):
    result = mixed / token_layout(total)
    return result.reshape(SEQS * SPAN, -1).astype(jnp.bfloat16)


def per_device(
    queries, new_keys, new_values, cache_keys, cache_values, out_weight, residual, norm_gain
):
    tp_size = lax.axis_size("tp")
    paired = tp_size == 2 * KVH
    local_kv = 1 if paired else cache_keys.shape[1] // CTX
    parity = lax.axis_index("tp") % 2

    def join_dims(own_piece, other_piece):
        first = jnp.concatenate([own_piece, other_piece], axis=-1)
        second = jnp.concatenate([other_piece, own_piece], axis=-1)
        return jnp.where(parity == 0, first, second)

    if paired:
        other_keys, other_values, other_stored_keys, other_stored_values = partner(
            (new_keys, new_values, cache_keys, cache_values), "tp", 0
        )
        fresh_keys = join_dims(new_keys, other_keys)
        fresh_values = join_dims(new_values, other_values)
        stored_keys = jnp.concatenate([cache_keys, other_stored_keys], axis=1)
        stored_values = jnp.concatenate([cache_values, other_stored_values], axis=1)
    else:
        fresh_keys, fresh_values = (new_keys, new_values)
        stored_keys, stored_values = (cache_keys, cache_values)
    mixed, peak, total = attend_block(
        queries, stored_keys, stored_values, fresh_keys, fresh_values, local_kv
    )
    attended = finish_rows(mixed, total)
    projected = lax.psum_scatter(
        lax.dot_general(
            out_weight, attended, (((0,), (1,)), ((), ())), preferred_element_type=jnp.float32
        ).astype(jnp.bfloat16),
        "tp",
        scatter_dimension=0,
        tiled=True,
    ).astype(jnp.float32)
    hidden = residual.astype(jnp.float32) + jnp.transpose(projected)
    squares = lax.psum(jnp.sum(hidden * hidden, axis=1), "tp")
    scaled = (
        hidden * lax.rsqrt(squares / D + EPSILON)[:, None] * norm_gain.astype(jnp.float32)[None, :]
    )
    return scaled.astype(jnp.bfloat16)


SEQS_PER_PART = 1
HEADS_PER_BLOCK = 2
KEY_CHUNK = 1024
PIECES = 4
MASKED = -1e30
LOG2E = 1.4426950408889634
MESH = pl.DeviceIdType.MESH


def lane_max(tile, running):
    for start in range(0, tile.shape[1], 128):
        part = tile[:, start : start + 128]
        running = part if running is None else jnp.maximum(running, part)
    return running


def attend_step(row, q_ref, k_ref, v_ref, nk_ref, nv_ref, att_ref, vx_ref, slots, column):
    stored = k_ref.shape[1]
    groups = q_ref.shape[1] // HD
    rows = HEADS_PER_BLOCK * SPAN
    blocks = groups // HEADS_PER_BLOCK
    vx_ref[0:stored, 0:HD] = v_ref[0]
    vx_ref[stored : stored + SPAN, 0:HD] = nv_ref[...]
    factor = HD ** (-0.5) * LOG2E
    chunks = [(start, KEY_CHUNK) for start in range(0, stored, KEY_CHUNK)] + [(stored, SPAN)]
    position = lax.broadcasted_iota(jnp.int32, (SPAN, SPAN), 0)
    causal_one = position >= lax.broadcasted_iota(jnp.int32, (SPAN, SPAN), 1)
    causal = jnp.concatenate([causal_one] * HEADS_PER_BLOCK, axis=0)

    def score_chunk(block, start, size, running):
        first = block * HEADS_PER_BLOCK
        heads = [q_ref[:, (first + i) * HD : (first + i + 1) * HD] for i in range(HEADS_PER_BLOCK)]
        q = heads[0] if len(heads) == 1 else jnp.concatenate(heads, axis=0)
        keys = nk_ref[...] if start == stored else k_ref[0, start : start + size, :]
        tile = lax.dot_general(
            q, keys, (((1,), (1,)), ((), ())), preferred_element_type=jnp.float32
        )
        if start == stored:
            tile = jnp.where(causal, tile, MASKED)
        slots[block % 2][:, start : start + size] = tile
        return lane_max(tile, running)

    running = None
    for start, size in chunks:
        running = score_chunk(0, start, size, running)
    for block in range(blocks):
        peak = jnp.max(running, axis=1, keepdims=True)
        running = None
        total = None
        for start, size in chunks:
            if block + 1 < blocks:
                running = score_chunk(block + 1, start, size, running)
            weights = jnp.exp2((slots[block % 2][:, start : start + size] - peak) * factor)
            term = jnp.dot(
                weights.astype(jnp.bfloat16),
                vx_ref[start : start + size, :],
                preferred_element_type=jnp.float32,
            )
            total = term if total is None else total + term
        result = (total[:, :HD] / total[:, HD:]).astype(jnp.bfloat16)
        for i in range(HEADS_PER_BLOCK):
            where = column + (block * HEADS_PER_BLOCK + i) * HD
            att_ref[pl.ds(row, SPAN), pl.ds(where, HD)] = result[i * SPAN : (i + 1) * SPAN]


def fused_kernel(
    q_ref, k_ref, v_ref, nk_ref, nv_ref, w_hbm, res_ref, gain_ref, out_hbm,
    w_ref, att_ref, vx_ref, score_a, score_b,
    s1_send, s1_recv, s2_send, s2_recv, hidden, staged, sq_send, sq_recv,
    w_sem, s1_ss, s1_rs, s2_ss, s2_rs, sq_ss, sq_rs, out_sem,
):
    s, g = pl.program_id(0), pl.program_id(1)
    local_kv = pl.num_programs(1)
    parts = SEQS // SEQS_PER_PART
    tokens = SEQS_PER_PART * SPAN
    width = hidden.shape[2]
    piece = width // PIECES
    me = lax.axis_index("tp")
    chip, core = me // 2, me % 2
    sibling = chip * 2 + (1 - core)
    across = (1 - chip) * 2 + core
    diagonal = (1 - chip) * 2 + (1 - core)
    w_pieces = w_sem.shape[0]
    w_rows = w_ref.shape[0] // w_pieces

    def w_copy(i):
        span = pl.ds(i * w_rows, w_rows)
        return pltpu.make_async_copy(w_hbm.at[span], w_ref.at[span], w_sem.at[i])

    def remote(src, dst, ss, rs, device):
        return pltpu.make_async_remote_copy(
            src_ref=src, dst_ref=dst, send_sem=ss, recv_sem=rs,
            device_id={"tp": device}, device_id_type=MESH,
        )

    def stage1(p, which, j):
        col = pl.ds(which * width + j * piece, piece)
        k = which * PIECES + j
        return remote(
            s1_send.at[:, col], s1_recv.at[p % 2, :, col], s1_ss.at[k], s1_rs.at[p % 2, k], sibling
        )

    def stage2(p, j):
        col = pl.ds(j * piece, piece)
        return remote(
            s2_send.at[:, col], s2_recv.at[p % 2, :, col], s2_ss.at[j], s2_rs.at[p % 2, j], across
        )

    def squares(p):
        return [
            remote(sq_send.at[p], sq_recv.at[p, i], sq_ss.at[p, i], sq_rs.at[p, i], device)
            for i, device in enumerate((sibling, across, diagonal))
        ]

    def out_copy(p):
        return pltpu.make_async_copy(
            staged.at[p % 2], out_hbm.at[pl.ds(p * tokens, tokens)], out_sem.at[p % 2]
        )

    @pl.when((s == 0) & (g == 0))
    def _():
        barrier = pltpu.get_barrier_semaphore()
        for device in (sibling, across, diagonal):
            pl.semaphore_signal(barrier, inc=1, device_id={"tp": device}, device_id_type=MESH)
        for i in range(w_pieces):
            w_copy(i).start()
        vx_ref[:, HD:] = jnp.ones((vx_ref.shape[0], vx_ref.shape[1] - HD), jnp.bfloat16)
        pl.semaphore_wait(barrier, 3)

    attend_step(
        pl.multiple_of(lax.rem(s, SEQS_PER_PART) * SPAN, SPAN),
        q_ref, k_ref, v_ref, nk_ref, nv_ref, att_ref, vx_ref, (score_a, score_b),
        pl.multiple_of(g * q_ref.shape[1], 128),
    )

    def project(owner, j):
        col = pl.multiple_of(owner * width + j * piece, 128)
        return jnp.dot(
            att_ref[...], w_ref[:, pl.ds(col, piece)], preferred_element_type=jnp.float32
        )

    def project_part(p):
        for j in range(PIECES):
            s1_send[:, j * piece : (j + 1) * piece] = project(diagonal, j).astype(jnp.bfloat16)
            stage1(p, 0, j).start()
            own = project(across, j)
            stage1(p, 0, j).wait_recv()
            both = own + s1_recv[p % 2, :, j * piece : (j + 1) * piece].astype(jnp.float32)
            s2_send[:, j * piece : (j + 1) * piece] = both.astype(jnp.bfloat16)
            stage2(p, j).start()
        for j in range(PIECES):
            col = slice(width + j * piece, width + (j + 1) * piece)
            s1_send[:, col] = project(sibling, j).astype(jnp.bfloat16)
            stage1(p, 1, j).start()
            own = slice(j * piece, (j + 1) * piece)
            hidden[p % 2, :, own] = project(me, j) + res_ref[:, own].astype(jnp.float32)

    def collect(p):
        for j in range(PIECES):
            stage1(p, 0, j).wait_send()
            stage1(p, 1, j).wait()
        lanes = None
        for j in range(PIECES):
            stage2(p, j).wait()
            col = slice(j * piece, (j + 1) * piece)
            other = slice(width + j * piece, width + (j + 1) * piece)
            value = (
                hidden[p % 2, :, col]
                + s1_recv[p % 2, :, other].astype(jnp.float32)
                + s2_recv[p % 2, :, col].astype(jnp.float32)
            )
            hidden[p % 2, :, col] = value
            for start in range(0, piece, 128):
                tile = value[:, start : start + 128]
                lanes = tile * tile if lanes is None else lanes + tile * tile
        for i in range(SEQS_PER_PART):
            turned = jnp.transpose(lanes[i * SPAN : (i + 1) * SPAN])
            row = jnp.sum(turned, axis=0, keepdims=True)
            sq_send[p, :, i * SPAN : (i + 1) * SPAN] = jnp.broadcast_to(row, (8, SPAN))
        for copy in squares(p):
            copy.start()

    def finish(p):
        for copy in squares(p):
            copy.wait()
        summed = sq_send[p] + sq_recv[p, 0] + sq_recv[p, 1] + sq_recv[p, 2]
        for i in range(SEQS_PER_PART):
            row = summed[0:1, i * SPAN : (i + 1) * SPAN]
            power = jnp.transpose(jnp.broadcast_to(row, (SPAN, SPAN))) / D
            scale = lax.rsqrt(power + EPSILON)
            for start in range(0, width, 128):
                value = hidden[p % 2, i * SPAN : (i + 1) * SPAN, start : start + 128]
                scaled = value * scale * gain_ref[:, start : start + 128].astype(jnp.float32)
                staged[p % 2, i * SPAN : (i + 1) * SPAN, start : start + 128] = scaled.astype(
                    jnp.bfloat16
                )
        out_copy(p).start()

    p = s // SEQS_PER_PART

    @pl.when((lax.rem(s, SEQS_PER_PART) == SEQS_PER_PART - 1) & (g == local_kv - 1))
    def _():
        @pl.when(p == 0)
        def _():
            for i in range(w_pieces):
                w_copy(i).wait()

        @pl.when(p > 0)
        def _():
            collect(p - 1)

        project_part(p)

        @pl.when(p > 2)
        def _():
            out_copy(p - 3).wait()

        @pl.when(p > 0)
        def _():
            finish(p - 1)

        @pl.when(p == parts - 1)
        def _():
            collect(p)
            if parts > 2:
                out_copy(p - 2).wait()
            finish(p)
            if parts > 1:
                out_copy(p - 1).wait()
            out_copy(p).wait()


def fused(queries, new_keys, new_values, cache_keys, cache_values, out_weight, residual, norm_gain):
    length = cache_keys.shape[1] // (new_keys.shape[1] // HD)
    local_kv = new_keys.shape[1] // HD
    group_width = queries.shape[1] // local_kv
    width = residual.shape[1]
    parts = SEQS // SEQS_PER_PART
    tokens = SEQS_PER_PART * SPAN
    keys_all = length + SPAN
    rows = HEADS_PER_BLOCK * SPAN
    bf16, f32 = jnp.bfloat16, jnp.float32
    dma = pltpu.SemaphoreType.DMA
    return pl.pallas_call(
        fused_kernel,
        grid=(SEQS, local_kv),
        out_shape=jax.ShapeDtypeStruct(residual.shape, bf16),
        in_specs=[
            pl.BlockSpec((SPAN, group_width), lambda s, g: (s, g)),
            pl.BlockSpec((1, length, HD), lambda s, g: (s, g, 0)),
            pl.BlockSpec((1, length, HD), lambda s, g: (s, g, 0)),
            pl.BlockSpec((SPAN, HD), lambda s, g: (s, g)),
            pl.BlockSpec((SPAN, HD), lambda s, g: (s, g)),
            pl.BlockSpec(memory_space=pl.ANY),
            pl.BlockSpec((tokens, width), lambda s, g: (s // SEQS_PER_PART, 0)),
            pl.BlockSpec((1, width), lambda s, g: (0, 0)),
        ],
        out_specs=pl.BlockSpec(memory_space=pl.ANY),
        scratch_shapes=[
            pltpu.VMEM(out_weight.shape, bf16),
            pltpu.VMEM((tokens, queries.shape[1]), bf16),
            pltpu.VMEM((keys_all, 2 * HD), bf16),
            pltpu.VMEM((rows, keys_all), f32),
            pltpu.VMEM((rows, keys_all), f32),
            pltpu.VMEM((tokens, 2 * width), bf16),
            pltpu.VMEM((2, tokens, 2 * width), bf16),
            pltpu.VMEM((tokens, width), bf16),
            pltpu.VMEM((2, tokens, width), bf16),
            pltpu.VMEM((2, tokens, width), f32),
            pltpu.VMEM((2, tokens, width), bf16),
            pltpu.VMEM((parts, 8, tokens), f32),
            pltpu.VMEM((parts, 3, 8, tokens), f32),
            dma((8,)),
            dma((2 * PIECES,)),
            dma((2, 2 * PIECES)),
            dma((PIECES,)),
            dma((2, PIECES)),
            dma((parts, 3)),
            dma((parts, 3)),
            dma((2,)),
        ],
        compiler_params=pltpu.CompilerParams(
            collective_id=0,
            has_side_effects=True,
            vmem_limit_bytes=67043328,
            dimension_semantics=("arbitrary", "arbitrary"),
        ),
    )(
        queries, cache_keys, cache_values, new_keys, new_values, out_weight, residual,
        norm_gain.reshape(1, -1),
    )


def solution(mesh):
    in_specs = (
        P("dp", "tp"),
        P("dp", "tp"),
        P("dp", "tp"),
        P("dp", "tp", None),
        P("dp", "tp", None),
        P("tp", None),
        P("dp", "tp"),
        P("tp"),
    )
    out_specs = P("dp", "tp")
    return jax.shard_map(
        fused if mesh.shape["tp"] == 4 else per_device, mesh=mesh, in_specs=in_specs, out_specs=out_specs, check_vma=False
    )
```

profile of v0, /device:TPU:0, one launch (start us, length us, event | category | flops | bytes accessed | tf_op | source)
XLA Modules:
  0.0 107.5 jit_solution(1877327550477731214)
XLA Ops:
  0.0 1.3 %reshape.3.gain_ref = bf16[1,2048]{1,0:T(2,128)(2,1)} reshape(bf16[2048]{0:T(1024)(128)(2,1)} %param.15) | data formatting | bytes 8192 | tf_op jit(solution)/shard_map/reshape | solution.py:410
  1.3 103.0 %shard_map.82 = bf16[512,2048]{1,0:T(8,128)(2,1)} custom-call(bf16[512,2048]{1,0:T(8,128)(2,1)} %q_ref.1, bf16[4,8192,128]{2,1,0:T(8,128)(2,1)} %k_ref.1, bf16[4,8192,128]{2,1,0:T(8,128)(2,1)} %v_ref.1, bf16[512,256]{1,0:T(8,128)(2,1)} %nk_ref.1, bf16[512,256]{1,0:T(8,128)(2,1)} %nv_ref.1, bf16[2048,8192]{1,0:T(8,128)(2,1)} %w_hbm.1, ...), custom_call_target="tpu_custom_call" | custom-call | tf_op jit(solution)/shard_map/pallas_call | solution.py:364
  104.3 3.2 %copy.10 = bf16[512,2048]{1,0:T(8,128)(2,1)} copy(bf16[512,2048]{1,0:T(8,128)(2,1)} %shard_map.82) | data formatting | bytes 4194304
where the time goes:
time: 108 us; the launch traced here: 107 us
  Pallas kernels  103 us (95%)
  local copies, waits for them, and re-layouts  4.45 us (4%)
    pallas_call x1, Pallas kernels, fused(): pl.pallas_call(fused_kernel, grid=(SEQS, local_kv), out_shape=jax.ShapeDt...  103 us
    unnamed x1, local copies, waits for them, and re-layouts  3.16 us

commit v1 on v0

v1 whole, which is shorter than its diff:
```python
import functools

import jax
import jax.numpy as jnp
from jax import lax
from jax.experimental import pallas as pl
from jax.experimental.pallas import tpu as pltpu
from jax.sharding import PartitionSpec as P

D = 8192
KVH = 8
HD = 128
SPAN = 128
SEQS = 4
CTX = 4096


EPSILON = 1e-05


def partner(value, axis, bit):
    mask = 2**bit
    pairs = [(source, source ^ mask) for source in range(lax.axis_size(axis))]
    return lax.ppermute(value, axis, pairs)


def attend_block(query_rows, stored_keys, stored_values, fresh_keys, fresh_values, local_kv):
    heads_here = query_rows.shape[1] // HD
    groups = heads_here // local_kv
    length = stored_keys.shape[1] // local_kv
    scaling = HD ** (-0.5)
    grouped = query_rows.reshape(SEQS, SPAN, local_kv, groups, HD)
    old_keys = stored_keys.reshape(SEQS, local_kv, length, HD)
    old_values = stored_values.reshape(SEQS, local_kv, length, HD)
    scores = (
        jnp.einsum("sighd,sgjd->sghij", grouped, old_keys, preferred_element_type=jnp.float32)
        * scaling
    )
    peak = jnp.max(scores, axis=-1)
    recent_keys = fresh_keys.reshape(SEQS, SPAN, local_kv, HD)
    recent_values = fresh_values.reshape(SEQS, SPAN, local_kv, HD)
    recent_scores = (
        jnp.einsum("sighd,sjgd->sghij", grouped, recent_keys, preferred_element_type=jnp.float32)
        * scaling
    )
    causal = jnp.arange(SPAN)[:, None] >= jnp.arange(SPAN)[None, :]
    recent_scores = jnp.where(causal, recent_scores, -jnp.inf)
    peak = jnp.maximum(peak, jnp.max(recent_scores, axis=-1))
    weights = jnp.exp(scores - peak[..., None])
    total = jnp.sum(weights, axis=-1)
    mixed = jnp.einsum(
        "sghij,sgjd->sighd",
        weights.astype(jnp.bfloat16),
        old_values,
        preferred_element_type=jnp.float32,
    )
    recent_weights = jnp.exp(recent_scores - peak[..., None])
    total = total + jnp.sum(recent_weights, axis=-1)
    mixed = mixed + jnp.einsum(
        "sghij,sjgd->sighd",
        recent_weights.astype(jnp.bfloat16),
        recent_values,
        preferred_element_type=jnp.float32,
    )
    return (mixed, peak, total)


def token_layout(stat):
    return jnp.transpose(stat, (0, 3, 1, 2))[..., None]


def finish_rows(mixed, total):
    result = mixed / token_layout(total)
    return result.reshape(SEQS * SPAN, -1).astype(jnp.bfloat16)


def per_device(
    queries, new_keys, new_values, cache_keys, cache_values, out_weight, residual, norm_gain
):
    tp_size = lax.axis_size("tp")
    paired = tp_size == 2 * KVH
    local_kv = 1 if paired else cache_keys.shape[1] // CTX
    parity = lax.axis_index("tp") % 2

    def join_dims(own_piece, other_piece):
        first = jnp.concatenate([own_piece, other_piece], axis=-1)
        second = jnp.concatenate([other_piece, own_piece], axis=-1)
        return jnp.where(parity == 0, first, second)

    if paired:
        other_keys, other_values, other_stored_keys, other_stored_values = partner(
            (new_keys, new_values, cache_keys, cache_values), "tp", 0
        )
        fresh_keys = join_dims(new_keys, other_keys)
        fresh_values = join_dims(new_values, other_values)
        stored_keys = jnp.concatenate([cache_keys, other_stored_keys], axis=1)
        stored_values = jnp.concatenate([cache_values, other_stored_values], axis=1)
    else:
        fresh_keys, fresh_values = (new_keys, new_values)
        stored_keys, stored_values = (cache_keys, cache_values)
    mixed, peak, total = attend_block(
        queries, stored_keys, stored_values, fresh_keys, fresh_values, local_kv
    )
    attended = finish_rows(mixed, total)
    projected = lax.psum_scatter(
        lax.dot_general(
            out_weight, attended, (((0,), (1,)), ((), ())), preferred_element_type=jnp.float32
        ).astype(jnp.bfloat16),
        "tp",
        scatter_dimension=0,
        tiled=True,
    ).astype(jnp.float32)
    hidden = residual.astype(jnp.float32) + jnp.transpose(projected)
    squares = lax.psum(jnp.sum(hidden * hidden, axis=1), "tp")
    scaled = (
        hidden * lax.rsqrt(squares / D + EPSILON)[:, None] * norm_gain.astype(jnp.float32)[None, :]
    )
    return scaled.astype(jnp.bfloat16)


HEADS_PER_BLOCK = 2
KEY_CHUNK = 1024
CHAINS = 32
PIECES = 4
MASKED = -1e30
LOG2E = 1.4426950408889634
MESH = pl.DeviceIdType.MESH


def attend_step(row, q_ref, k_ref, v_ref, nk_ref, nv_ref, att_ref, vt_ref, qx_ref, slots, column):
    stored = k_ref.shape[1]
    groups = q_ref.shape[1] // HD
    lanes = HEADS_PER_BLOCK * SPAN
    blocks = groups // HEADS_PER_BLOCK
    factor = HD ** (-0.5) * LOG2E
    chunks = [(start, KEY_CHUNK) for start in range(0, stored, KEY_CHUNK)] + [(stored, SPAN)]
    key = lax.broadcasted_iota(jnp.int32, (SPAN, SPAN), 0)
    causal_one = key <= lax.broadcasted_iota(jnp.int32, (SPAN, SPAN), 1)
    causal = jnp.concatenate([causal_one] * HEADS_PER_BLOCK, axis=1)

    def turn_values(start, size):
        values = nv_ref[...] if start == stored else v_ref[0, start : start + size, :]
        vt_ref[:, start : start + size] = jnp.transpose(values)

    def load_queries(block):
        for i in range(HEADS_PER_BLOCK):
            where = (block * HEADS_PER_BLOCK + i) * HD
            scaled = jnp.transpose(q_ref[:, where : where + HD].astype(jnp.float32)) * factor
            high = scaled.astype(jnp.bfloat16)
            low = (scaled - high.astype(jnp.float32)).astype(jnp.bfloat16)
            tokens = slice(i * SPAN, (i + 1) * SPAN)
            qx_ref[block % 2, 0:HD, tokens] = high
            qx_ref[block % 2, HD : 2 * HD, tokens] = low

    def score_chunk(block, start, size, running):
        keys = nk_ref[...] if start == stored else k_ref[0, start : start + size, :]
        tile = jnp.dot(
            jnp.concatenate([keys, keys], axis=1), qx_ref[block % 2],
            preferred_element_type=jnp.float32,
        )
        if start == stored:
            tile = jnp.where(causal, tile, MASKED)
        slots[block % 2][start : start + size, :] = tile
        peak = jnp.max(tile.reshape(size // CHAINS, CHAINS, lanes), axis=0)
        return peak if running is None else jnp.maximum(running, peak)

    def halves(start, size):
        if size < 2 * SPAN:
            return [(start, size)]
        return [(start, size // 2), (start + size // 2, size // 2)]

    def score_halves(block, start, size, running):
        for first, part in halves(start, size):
            running = score_chunk(block, first, part, running)
        return running

    running = None
    load_queries(0)
    for start, size in chunks:
        turn_values(start, size)
        running = score_halves(0, start, size, running)
    for block in range(blocks):
        peak = jnp.max(running, axis=0, keepdims=True)
        running, total, mixed = None, None, [None, None]
        if block + 1 < blocks:
            load_queries(block + 1)
        for start, size in chunks:
            if block + 1 < blocks:
                running = score_halves(block + 1, start, size, running)
            for which, (first, part) in enumerate(halves(start, size)):
                weights = jnp.exp2(slots[block % 2][first : first + part, :] - peak)
                summed = jnp.sum(weights.reshape(part // CHAINS, CHAINS, lanes), axis=0)
                total = summed if total is None else total + summed
                term = jnp.dot(
                    vt_ref[:, first : first + part],
                    weights.astype(jnp.bfloat16),
                    preferred_element_type=jnp.float32,
                )
                mixed[which] = term if mixed[which] is None else mixed[which] + term
        result = (mixed[0] + mixed[1]) * (1.0 / jnp.sum(total, axis=0, keepdims=True))
        for i in range(HEADS_PER_BLOCK):
            where = column + (block * HEADS_PER_BLOCK + i) * HD
            turned = jnp.transpose(result[:, i * SPAN : (i + 1) * SPAN])
            att_ref[pl.ds(row, SPAN), pl.ds(where, HD)] = turned.astype(jnp.bfloat16)


def fused_kernel(
    q_ref, k_ref, v_ref, nk_ref, nv_ref, w_hbm, res_hbm, gain_ref, out_hbm,
    w_ref, att_ref, vt_ref, qx_ref, score_a, score_b, res_ref,
    s1_send, s1_recv, s2_send, s2_recv, own_send, own_recv, sq_send, sq_recv,
    w_sem, res_sem, s1_ss, s1_rs, s2_ss, s2_rs, own_ss, own_rs, sq_ss, sq_rs, out_sem,
):
    s, g = pl.program_id(0), pl.program_id(1)
    parts, local_kv = pl.num_programs(0), pl.num_programs(1)
    width = res_ref.shape[1]
    piece = width // PIECES
    block = score_a.shape[1]
    everyone = SEQS * SPAN
    me = lax.axis_index("tp")
    chip, core = me // 2, me % 2
    sibling = chip * 2 + (1 - core)
    across = (1 - chip) * 2 + core
    diagonal = (1 - chip) * 2 + (1 - core)

    owners = (diagonal, across, sibling, me)

    def w_place(which, j):
        return pl.ds(which % 3 * width + j * piece, piece)

    def w_copy(which, j):
        col = pl.ds(pl.multiple_of(owners[which] * width + j * piece, 128), piece)
        return pltpu.make_async_copy(
            w_hbm.at[:, col], w_ref.at[:, w_place(which, j)], w_sem.at[which * PIECES + j]
        )

    def res_copy():
        return pltpu.make_async_copy(res_hbm, res_ref, res_sem.at[0])

    def remote(src, dst, ss, rs, device):
        return pltpu.make_async_remote_copy(
            src_ref=src, dst_ref=dst, send_sem=ss, recv_sem=rs,
            device_id={"tp": device}, device_id_type=MESH,
        )

    def stage1(p, j):
        col = pl.ds(j * piece, piece)
        return remote(
            s1_send.at[p % 2, :, col], s1_recv.at[p % 2, :, col],
            s1_ss.at[p % 2, j], s1_rs.at[p % 2, j], sibling,
        )

    def stage2(p, j):
        at = (pl.ds(pl.multiple_of(p * SPAN, SPAN), SPAN), pl.ds(j * piece, piece))
        return remote(s2_send.at[at], s2_recv.at[at], s2_ss.at[p, j], s2_rs.at[p, j], across)

    def own(j):
        col = pl.ds(j * piece, piece)
        return remote(own_send.at[:, col], own_recv.at[:, col], own_ss.at[j], own_rs.at[j], sibling)

    def squares(p):
        return [
            remote(sq_send.at[p], sq_recv.at[p, i], sq_ss.at[p, i], sq_rs.at[p, i], device)
            for i, device in enumerate((sibling, across, diagonal))
        ]

    def out_copy(p):
        rows = pl.ds(p * SPAN, SPAN)
        return pltpu.make_async_copy(att_ref.at[rows], out_hbm.at[rows], out_sem.at[p])

    @pl.when((s == 0) & (g == 0))
    def _():
        barrier = pltpu.get_barrier_semaphore()
        for device in (sibling, across, diagonal):
            pl.semaphore_signal(barrier, inc=1, device_id={"tp": device}, device_id_type=MESH)
        for which in range(2):
            for j in range(PIECES):
                w_copy(which, j).start()
        pl.semaphore_wait(barrier, 3)

    @pl.when((s == 1) & (g == 0))
    def _():
        for j in range(PIECES):
            w_copy(2, j).start()
        res_copy().start()

    attend_step(
        pl.multiple_of(s * SPAN, SPAN),
        q_ref, k_ref, v_ref, nk_ref, nv_ref, att_ref, vt_ref, qx_ref, (score_a, score_b),
        pl.multiple_of(g * q_ref.shape[1], 128),
    )

    def project(rows, which, j):
        return jnp.dot(
            att_ref[rows, :], w_ref[:, w_place(which, j)], preferred_element_type=jnp.float32
        )

    @pl.when(g == local_kv - 1)
    def _():
        rows = pl.ds(pl.multiple_of(s * SPAN, SPAN), SPAN)

        @pl.when(s == 0)
        def _():
            for which in range(2):
                for j in range(PIECES):
                    w_copy(which, j).wait()

        @pl.when(s > 1)
        def _():
            for j in range(PIECES):
                stage1(s - 2, j).wait_send()

        for j in range(PIECES):
            s1_send[s % 2, :, j * piece : (j + 1) * piece] = project(rows, 0, j).astype(
                jnp.bfloat16
            )
            stage1(s, j).start()

        @pl.when(s == parts - 1)
        def _():
            for j in range(PIECES):
                w_copy(3, j).start()

        for j in range(PIECES):
            near = project(rows, 1, j)
            stage1(s, j).wait_recv()
            col = slice(j * piece, (j + 1) * piece)
            both = near + s1_recv[s % 2, :, col].astype(jnp.float32)
            s2_send[rows, col] = both.astype(jnp.bfloat16)
            stage2(s, j).start()

    def held(p, start):
        first = (start // block) * everyone + p * SPAN
        return (slice(first, first + SPAN), slice(start % block, start % block + 128))

    def collect(p):
        for j in range(PIECES):
            stage2(p, j).wait()
        rows = slice(p * SPAN, (p + 1) * SPAN)
        lanes = None
        for start in range(0, width, 128):
            col = slice(start, start + 128)
            value = (
                score_a[held(p, start)]
                + own_recv[rows, col].astype(jnp.float32)
                + s2_recv[rows, col].astype(jnp.float32)
            )
            score_a[held(p, start)] = value
            lanes = value * value if lanes is None else lanes + value * value
        row = jnp.sum(jnp.transpose(lanes), axis=0, keepdims=True)
        sq_send[p] = jnp.broadcast_to(row, (8, SPAN))
        for copy in squares(p):
            copy.start()

    def finish(p):
        for copy in squares(p):
            copy.wait()
        summed = sq_send[p] + sq_recv[p, 0] + sq_recv[p, 1] + sq_recv[p, 2]
        power = jnp.transpose(jnp.broadcast_to(summed[0:1, :], (SPAN, SPAN))) / D
        scale = lax.rsqrt(power + EPSILON)
        for start in range(0, width, 128):
            gain = gain_ref[:, start : start + 128].astype(jnp.float32)
            scaled = score_a[held(p, start)] * scale * gain
            att_ref[p * SPAN : (p + 1) * SPAN, start : start + 128] = scaled.astype(jnp.bfloat16)
        out_copy(p).start()

    @pl.when((s == parts - 1) & (g == local_kv - 1))
    def _():
        for j in range(PIECES):
            w_copy(2, j).wait()
        res_copy().wait()
        for j in range(PIECES):
            own_send[:, j * piece : (j + 1) * piece] = project(slice(None), 2, j).astype(
                jnp.bfloat16
            )
            own(j).start()
        for j in range(PIECES):
            w_copy(3, j).wait()
        for j in range(PIECES):
            result = project(slice(None), 3, j)
            for start in range(0, piece, block):
                first = (j * piece + start) // block * everyone
                score_a[first : first + everyone, :] = result[:, start : start + block] + res_ref[
                    :, j * piece + start : j * piece + start + block
                ].astype(jnp.float32)
        for j in range(PIECES):
            own(j).wait()
        for p in range(SEQS - 1):
            collect(p)
        for p in range(SEQS - 1):
            finish(p)
        collect(SEQS - 1)
        finish(SEQS - 1)
        for p in (SEQS - 2, SEQS - 1):
            for j in range(PIECES):
                stage1(p, j).wait_send()
        for p in range(SEQS):
            out_copy(p).wait()


def fused(queries, new_keys, new_values, cache_keys, cache_values, out_weight, residual, norm_gain):
    length = cache_keys.shape[1] // (new_keys.shape[1] // HD)
    local_kv = new_keys.shape[1] // HD
    group_width = queries.shape[1] // local_kv
    tokens, width = residual.shape
    keys_all = length + SPAN
    lanes = HEADS_PER_BLOCK * SPAN
    bf16, f32 = jnp.bfloat16, jnp.float32
    dma = pltpu.SemaphoreType.DMA
    return pl.pallas_call(
        fused_kernel,
        grid=(SEQS, local_kv),
        out_shape=jax.ShapeDtypeStruct(residual.shape, bf16),
        in_specs=[
            pl.BlockSpec((SPAN, group_width), lambda s, g: (s, g)),
            pl.BlockSpec((1, length, HD), lambda s, g: (s, g, 0)),
            pl.BlockSpec((1, length, HD), lambda s, g: (s, g, 0)),
            pl.BlockSpec((SPAN, HD), lambda s, g: (s, g)),
            pl.BlockSpec((SPAN, HD), lambda s, g: (s, g)),
            pl.BlockSpec(memory_space=pl.ANY),
            pl.BlockSpec(memory_space=pl.ANY),
            pl.BlockSpec((1, width), lambda s, g: (0, 0)),
        ],
        out_specs=pl.BlockSpec(memory_space=pl.ANY),
        scratch_shapes=[
            pltpu.VMEM((out_weight.shape[0], 3 * width), bf16),
            pltpu.VMEM((tokens, queries.shape[1]), bf16),
            pltpu.VMEM((HD, keys_all), bf16),
            pltpu.VMEM((2, lanes, 2 * HD), bf16),
            pltpu.VMEM((keys_all, lanes), f32),
            pltpu.VMEM((keys_all, lanes), f32),
            pltpu.VMEM((tokens, width), bf16),
            pltpu.VMEM((2, SPAN, width), bf16),
            pltpu.VMEM((2, SPAN, width), bf16),
            pltpu.VMEM((tokens, width), bf16),
            pltpu.VMEM((tokens, width), bf16),
            pltpu.VMEM((tokens, width), bf16),
            pltpu.VMEM((tokens, width), bf16),
            pltpu.VMEM((SEQS, 8, SPAN), f32),
            pltpu.VMEM((SEQS, 3, 8, SPAN), f32),
            dma((4 * PIECES,)),
            dma((1,)),
            dma((2, PIECES)),
            dma((2, PIECES)),
            dma((SEQS, PIECES)),
            dma((SEQS, PIECES)),
            dma((PIECES,)),
            dma((PIECES,)),
            dma((SEQS, 3)),
            dma((SEQS, 3)),
            dma((SEQS,)),
        ],
        compiler_params=pltpu.CompilerParams(
            collective_id=0,
            has_side_effects=True,
            vmem_limit_bytes=67043328,
            dimension_semantics=("arbitrary", "arbitrary"),
        ),
    )(
        queries, cache_keys, cache_values, new_keys, new_values, out_weight, residual,
        norm_gain.reshape(1, -1),
    )


def solution(mesh):
    in_specs = (
        P("dp", "tp"),
        P("dp", "tp"),
        P("dp", "tp"),
        P("dp", "tp", None),
        P("dp", "tp", None),
        P("tp", None),
        P("dp", "tp"),
        P("tp"),
    )
    out_specs = P("dp", "tp")
    return jax.shard_map(
        fused if mesh.shape["tp"] == 4 else per_device, mesh=mesh, in_specs=in_specs, out_specs=out_specs, check_vma=False
    )
```

time: 108 us -> 85.2 us (0.79)
  Pallas kernels: 103 us -> 80.6 us
    pallas_call x1, Pallas kernels: 103 us -> 80.6 us  [fused(): pl.pallas_call(fused_kernel, grid=(SEQS, local_kv), out_shape=jax.ShapeDt...]
where the time goes in v1:
time: 85.2 us; the launch traced here: 85.1 us
  Pallas kernels  80.6 us (95%)
  local copies, waits for them, and re-layouts  4.45 us (5%)
    pallas_call x1, Pallas kernels, fused(): pl.pallas_call(fused_kernel, grid=(SEQS, local_kv), out_shape=jax.ShapeDt...  80.6 us
    unnamed x1, local copies, waits for them, and re-layouts  3.16 us

profile of v1, /device:TPU:0, one launch (start us, length us, event | category | flops | bytes accessed | tf_op | source)
XLA Modules:
  0.0 85.1 jit_solution(5441540343346449205)
XLA Ops:
  0.0 1.3 %reshape.3.gain_ref = bf16[1,2048]{1,0:T(2,128)(2,1)} reshape(bf16[2048]{0:T(1024)(128)(2,1)} %param.15) | data formatting | bytes 8192 | tf_op jit(solution)/shard_map/reshape | solution.py:460
  1.3 80.6 %shard_map.82 = bf16[512,2048]{1,0:T(8,128)(2,1)} custom-call(bf16[512,2048]{1,0:T(8,128)(2,1)} %q_ref.1, bf16[4,8192,128]{2,1,0:T(8,128)(2,1)} %k_ref.1, bf16[4,8192,128]{2,1,0:T(8,128)(2,1)} %v_ref.1, bf16[512,256]{1,0:T(8,128)(2,1)} %nk_ref.1, bf16[512,256]{1,0:T(8,128)(2,1)} %nv_ref.1, bf16[2048,8192]{1,0:T(8,128)(2,1)} %w_hbm.1, ...), custom_call_target="tpu_custom_call" | custom-call | tf_op jit(solution)/shard_map/pallas_call | solution.py:409
  81.9 3.2 %copy.10 = bf16[512,2048]{1,0:T(8,128)(2,1)} copy(bf16[512,2048]{1,0:T(8,128)(2,1)} %shard_map.82) | data formatting | bytes 4194304

commit v2 on v1

--- a/solution.py
+++ b/solution.py
@@ -206,7 +206,7 @@
 
 def fused_kernel(
     q_ref, k_ref, v_ref, nk_ref, nv_ref, w_hbm, res_hbm, gain_ref, out_hbm,
-    w_ref, att_ref, vt_ref, qx_ref, score_a, score_b, res_ref,
+    w_ref, att_ref, vt_ref, qx_ref, score_a, score_b, res_ref, near_ref,
     s1_send, s1_recv, s2_send, s2_recv, own_send, own_recv, sq_send, sq_recv,
     w_sem, res_sem, s1_ss, s1_rs, s2_ss, s2_rs, own_ss, own_rs, sq_ss, sq_rs, out_sem,
 ):
@@ -314,17 +314,12 @@
                 jnp.bfloat16
             )
             stage1(s, j).start()
-
-        @pl.when(s == parts - 1)
-        def _():
-            for j in range(PIECES):
-                w_copy(3, j).start()
-
-        for j in range(PIECES):
-            near = project(rows, 1, j)
+        for j in range(PIECES):
+            near_ref[:, j * piece : (j + 1) * piece] = project(rows, 1, j)
+        for j in range(PIECES):
             stage1(s, j).wait_recv()
             col = slice(j * piece, (j + 1) * piece)
-            both = near + s1_recv[s % 2, :, col].astype(jnp.float32)
+            both = near_ref[:, col] + s1_recv[s % 2, :, col].astype(jnp.float32)
             s2_send[rows, col] = both.astype(jnp.bfloat16)
             stage2(s, j).start()
 
@@ -358,13 +353,15 @@
         power = jnp.transpose(jnp.broadcast_to(summed[0:1, :], (SPAN, SPAN))) / D
         scale = lax.rsqrt(power + EPSILON)
         for start in range(0, width, 128):
-            gain = gain_ref[:, start : start + 128].astype(jnp.float32)
+            gain = gain_ref[start : start + 128].astype(jnp.float32)[None, :]
             scaled = score_a[held(p, start)] * scale * gain
             att_ref[p * SPAN : (p + 1) * SPAN, start : start + 128] = scaled.astype(jnp.bfloat16)
         out_copy(p).start()
 
     @pl.when((s == parts - 1) & (g == local_kv - 1))
     def _():
+        for j in range(PIECES):
+            w_copy(3, j).start()
         for j in range(PIECES):
             w_copy(2, j).wait()
         res_copy().wait()
@@ -384,17 +381,34 @@
                 ].astype(jnp.float32)
         for j in range(PIECES):
             own(j).wait()
-        for p in range(SEQS - 1):
+        for p in range(SEQS):
             collect(p)
-        for p in range(SEQS - 1):
+        for p in range(SEQS):
             finish(p)
-        collect(SEQS - 1)
-        finish(SEQS - 1)
         for p in (SEQS - 2, SEQS - 1):
             for j in range(PIECES):
                 stage1(p, j).wait_send()
         for p in range(SEQS):
             out_copy(p).wait()
+
+
+def hand_over(in_hbm, out_hbm, held, in_sem, out_sem):
+    rows = held.shape[1]
+
+    def copies(i):
+        span = pl.ds(i * rows, rows)
+        return (
+            pltpu.make_async_copy(in_hbm.at[span], held.at[i], in_sem.at[i]),
+            pltpu.make_async_copy(held.at[i], out_hbm.at[span], out_sem.at[i]),
+        )
+
+    for i in range(SEQS):
+        copies(i)[0].start()
+    for i in range(SEQS):
+        copies(i)[0].wait()
+        copies(i)[1].start()
+    for i in range(SEQS):
+        copies(i)[1].wait()
 
 
 def fused(queries, new_keys, new_values, cache_keys, cache_values, out_weight, residual, norm_gain):
@@ -406,7 +420,7 @@
     lanes = HEADS_PER_BLOCK * SPAN
     bf16, f32 = jnp.bfloat16, jnp.float32
     dma = pltpu.SemaphoreType.DMA
-    return pl.pallas_call(
+    result = pl.pallas_call(
         fused_kernel,
         grid=(SEQS, local_kv),
         out_shape=jax.ShapeDtypeStruct(residual.shape, bf16),
@@ -418,7 +432,7 @@
             pl.BlockSpec((SPAN, HD), lambda s, g: (s, g)),
             pl.BlockSpec(memory_space=pl.ANY),
             pl.BlockSpec(memory_space=pl.ANY),
-            pl.BlockSpec((1, width), lambda s, g: (0, 0)),
+            pl.BlockSpec((width,), lambda s, g: (0,)),
         ],
         out_specs=pl.BlockSpec(memory_space=pl.ANY),
         scratch_shapes=[
@@ -429,6 +443,7 @@
             pltpu.VMEM((keys_all, lanes), f32),
             pltpu.VMEM((keys_all, lanes), f32),
             pltpu.VMEM((tokens, width), bf16),
+            pltpu.VMEM((SPAN, width), f32),
             pltpu.VMEM((2, SPAN, width), bf16),
             pltpu.VMEM((2, SPAN, width), bf16),
             pltpu.VMEM((tokens, width), bf16),
@@ -457,8 +472,17 @@
         ),
     )(
         queries, cache_keys, cache_values, new_keys, new_values, out_weight, residual,
-        norm_gain.reshape(1, -1),
-    )
+        norm_gain,
+    )
+    return pl.pallas_call(
+        hand_over,
+        out_shape=jax.ShapeDtypeStruct(result.shape, bf16),
+        in_specs=[pl.BlockSpec(memory_space=pl.ANY)],
+        out_specs=pl.BlockSpec(memory_space=pl.ANY),
+        scratch_shapes=[
+            pltpu.VMEM((SEQS, tokens // SEQS, width), bf16), dma((SEQS,)), dma((SEQS,)),
+        ],
+    )(result)
 
 
 def solution(mesh):

time: 85.2 us -> 77.9 us (0.914)
  local copies, waits for them, and re-layouts: 4.45 us -> 0 us
  Pallas kernels: 80.6 us -> 77.8 us
    pallas_call x1, Pallas kernels: 80.6 us -> 75.3 us  [fused(): pl.pallas_call(fused_kernel, grid=(SEQS, local_kv), out_shape=jax.ShapeDt...]
    unnamed x1 -> x0, local copies, waits for them, and re-layouts: 3.16 us -> none
    pallas_call x0 -> x1, Pallas kernels: none -> 2.42 us  [fused(): pl.pallas_call(hand_over, out_shape=jax.ShapeDtypeStruct(result.shape, bf...]
    reshape x1 -> x0, local copies, waits for them, and re-layouts: 1.29 us -> none  [fused(): norm_gain.reshape(1, -1)]
where the time goes in v2:
time: 77.9 us; the launch traced here: 77.8 us
  Pallas kernels  77.8 us (100%)
    pallas_call x1, Pallas kernels, fused(): pl.pallas_call(fused_kernel, grid=(SEQS, local_kv), out_shape=jax.ShapeDt...  75.3 us
    pallas_call x1, Pallas kernels, fused(): pl.pallas_call(hand_over, out_shape=jax.ShapeDtypeStruct(result.shape, bf...  2.42 us

profile of v2, /device:TPU:0, one launch (start us, length us, event | category | flops | bytes accessed | tf_op | source)
XLA Modules:
  0.0 77.8 jit_solution(9611602979357044048)
XLA Ops:
  0.0 75.3 %shard_map.82.in_hbm = bf16[512,2048]{1,0:T(8,128)(2,1)} custom-call(bf16[512,2048]{1,0:T(8,128)(2,1)} %q_ref.1, bf16[4,8192,128]{2,1,0:T(8,128)(2,1)} %k_ref.1, bf16[4,8192,128]{2,1,0:T(8,128)(2,1)} %v_ref.1, bf16[512,256]{1,0:T(8,128)(2,1)} %nk_ref.1, bf16[512,256]{1,0:T(8,128)(2,1)} %nv_ref.1, bf16[2048,8192]{1,0:T(8,128)(2,1)} %w_hbm.1, ...), custom_call_target="tpu_custom_call" | custom-call | tf_op jit(solution)/shard_map/pallas_call | solution.py:423
  75.3 2.4 %shard_map.83 = bf16[512,2048]{1,0:T(8,128)(2,1)} custom-call(bf16[512,2048]{1,0:T(8,128)(2,1)} %shard_map.82.in_hbm), custom_call_target="tpu_custom_call" | custom-call | tf_op jit(solution)/shard_map/pallas_call | solution.py:477
